TPU v7x, 32 devices: a whole 2x2x4 slice. The times are simulated.
32 devices in a mesh: row: 4 (over z), col: 8 (over y, x, core).
Axes of the slice: x: 2, y: 2, z: 4, core: 2. Of those that a mesh axis runs over, the one named last changes fastest.
Arguments:
- tri_panels: float32 [8192, 4096], P('row', 'col'), may hold values from -1 to 2, as said below
- rhs_rows: float32 [8192, 1024], P(('row', 'col')), may hold values from -6 to 6
Outputs:
- rhs_grid: float32 [8192, 1024], P('row', 'col')
Inputs may be any that keep to these rules, and one draw needn't show every extreme that they name: `tri_panels`: in L's row order the entries above the diagonal are zero and the diagonal entries are positive.
All inputs are finite; a program needn't handle non-finite values.
Results may differ from a plain program's by a relative error of at most 0.00011.
Values sent between devices are 32-bit elements; how exact they have to be, the bound alone decides.
A program may use at most 256 MiB of HBM per device.

v0:
```python
import jax
import jax.numpy as jnp
from jax import lax
from jax.sharding import PartitionSpec as P


def broadcast(block, axis, source):
    block = jnp.where(lax.axis_index(axis) == source, block, jnp.zeros_like(block))
    return lax.psum(block, axis)


def on_device(tri_panels, rhs_rows):
    row_count = lax.axis_size("row")
    col_count = lax.axis_size("col")
    row_position = lax.axis_index("row")
    col_position = lax.axis_index("col")
    local_rows, block_size = tri_panels.shape
    blocks = local_rows // block_size
    sub_rows = block_size // col_count
    parted = rhs_rows.reshape(blocks, sub_rows, rhs_rows.shape[1])
    state_rhs = lax.all_to_all(parted, "col", split_axis=2, concat_axis=1, tiled=True)
    identity_block = jnp.eye(block_size, dtype=jnp.float32)
    own_pieces = tri_panels.reshape(blocks, block_size, block_size)
    own_diag = lax.dynamic_index_in_dim(own_pieces, col_position // row_count, 0, keepdims=False)
    own_diag = jnp.where(col_position % row_count == row_position, own_diag, identity_block)
    own_inverse = jax.scipy.linalg.solve_triangular(own_diag, identity_block, lower=True)

    def advance(state_rhs, panel_cols, inverse_block, step_index, first_slot):
        count = blocks - first_slot
        owner_row = step_index % row_count
        slot_index = step_index // row_count
        pieces = panel_cols.reshape(count, block_size, block_size)
        current = lax.dynamic_index_in_dim(state_rhs, slot_index, 0, keepdims=False)
        local_solution = jnp.dot(
            inverse_block,
            current,
            precision=lax.Precision.HIGHEST,
            preferred_element_type=jnp.float32,
        )
        solution = broadcast(local_solution, "row", owner_row)
        stored = jnp.where(row_position == owner_row, solution, current)
        state_rhs = lax.dynamic_update_index_in_dim(state_rhs, stored, slot_index, 0)
        global_block = (first_slot + jnp.arange(count, dtype=jnp.int32)) * row_count + row_position
        product = jnp.einsum("sij,jc->sic", pieces, solution, precision=lax.Precision.HIGHEST)
        trailing = state_rhs[first_slot:]
        trailing = jnp.where(
            (global_block > step_index)[:, None, None], trailing - product, trailing
        )
        if first_slot > 0:
            return jnp.concatenate([state_rhs[:first_slot], trailing], 0)
        return trailing

    group_count = (col_count + row_count - 1) // row_count
    everything, inverses = (
        lax.all_gather(tri_panels, "col", axis=1, tiled=True),
        lax.all_gather(own_inverse, "col", axis=1, tiled=True),
    )
    for first_slot in range(group_count):
        begin_step = first_slot * row_count
        end_step = min(begin_step + row_count, col_count)
        own_rows = everything[first_slot * block_size :]

        def upfront_step(step_index, state_rhs, own_rows=own_rows, first_slot=first_slot):
            panel_cols = lax.dynamic_slice_in_dim(own_rows, step_index * block_size, block_size, 1)
            inverse_block = lax.dynamic_slice_in_dim(
                inverses, step_index * block_size, block_size, 1
            )
            return advance(state_rhs, panel_cols, inverse_block, step_index, first_slot)

        state_rhs = lax.fori_loop(begin_step, end_step, upfront_step, state_rhs)
    return state_rhs.reshape(local_rows, state_rhs.shape[2])


def solution(mesh):
    return jax.shard_map(
        on_device,
        mesh=mesh,
        in_specs=(P("row", "col"), P(("row", "col"), None)),
        out_specs=P("row", "col"),
        check_vma=False,
    )
```

profile of v0, /device:TPU:0, one launch (start us, length us, event | category | flops | bytes accessed | tf_op | source)
XLA Modules:
  0.0 599.4 jit_solution(16486143902981897702)
XLA Ops:
  8.7 8.0 %while.33 = (s32[]{:T(128)}, f32[512,512]{1,0:T(8,128)S(1)}, s32[4,2]{0,1:T(2,128)S(1)}, f32[4,128,128]{2,1,0:T(8,128)S(1)}, s32[]{:T(128)}) while((s32[]{:T(128)}, f32[512,512]{1,0:T(8,128)S(1)}, s32[4,2]{0,1:T(2,128)S(1)}, f32[4,128,128]{2,1,0:T(8,128)S(1)}, s32[]{:T(128)}) %tuple.81), condition=%wide.while_cond, body=%wide.while_body.sunk | while | flops 2 | bytes 131181 | solution.py:26
  16.7 39.3 %custom-call.4 = f32[4,128,128]{1,2,0:T(8,128)S(1)} custom-call(f32[4,128,128]{2,1,0:T(8,128)S(1)} %get-tuple-element.284), custom_call_target="InvertDiagBlocksLowerTriangular" | custom-call | tf_op jit(solution)/shard_map/jit(_solve_triangular)/triangular_solve | solution.py:26
  64.1 5.2 all-to-all-start
  69.3 20.5 %all-to-all-done = f32[8,1,32768]{2,1,0:T(1,128)S(1)} async-done(((f32[8,1,32768]{2,1,0:T(1,128)}), f32[8,1,32768]{2,1,0:T(1,128)S(1)}, u32[]{:S(2)}, u32[]{:S(2)}) %all-to-all-start) | async-done | bytes 1048608 | tf_op jit(solution)/shard_map/all_to_all | solution.py:21
  95.7 81.6 %all-gather.5.cloned.1.call-done = f32[2048,4096]{1,0:T(8,128)} async-done(((f32[2048,512]{1,0:T(8,128)}), f32[2048,4096]{1,0:T(8,128)}) %all-gather.5.cloned.1.call-update) | async-done | bytes 33554448 | tf_op jit(solution)/shard_map/all_gather | solution.py:55
  177.3 17.5 %slice.70 = f32[1536,4096]{1,0:T(8,128)} slice(f32[2048,4096]{1,0:T(8,128)} %all-gather.5.cloned.1.call-done), slice={[512:2048], [0:4096]} | slice | bytes 50331648 | tf_op jit(solution)/shard_map/slice | solution.py:61
  194.7 39.0 %all-gather.3.cloned.1.call-done = f32[512,4096]{1,0:T(8,128)} async-done(((f32[512,512]{1,0:T(8,128)}), f32[512,4096]{1,0:T(8,128)}) %all-gather.3.cloned.1.call-update) | async-done | bytes 8388624 | tf_op jit(solution)/shard_map/all_gather | solution.py:56
  233.7 176.9 %while.31 = (s32[]{:T(128)}, f32[4,512,128]{2,1,0:T(8,128)S(1)}, s32[]{:T(128)}, f32[512,4096]{1,0:T(8,128)}, f32[2048,4096]{1,0:T(8,128)}, /*index=5*/s32[]{:T(...) while((s32[]{:T(128)}, f32[4,512,128]{2,1,0:T(8,128)S(1)}, ...), condition=%wide.region_2.3_spmd, body=%wide.region_0.2_spmd.sunk | while | flops 2013986816 | bytes 19399112 | solution.py:70
  236.7 4.6 constant_dynamic-slice_fusion.11
  241.4 31.1 %all-reduce.3.cloned.1.call-done = f32[512,128]{1,0:T(8,128)} async-done(((f32[512,128]{1,0:T(8,128)}), f32[512,128]{1,0:T(8,128)}) %all-reduce.3.cloned.1.call-update) | async-done | bytes 262160 | tf_op jit(solution)/shard_map/while/body/eval_jaxpr/psum | solution.py:9
  273.5 5.2 subtract_select_fusion.2
  281.8 4.6 constant_dynamic-slice_fusion.11
  286.4 30.0 %all-reduce.3.cloned.1.call-done = f32[512,128]{1,0:T(8,128)} async-done(((f32[512,128]{1,0:T(8,128)}), f32[512,128]{1,0:T(8,128)}) %all-reduce.3.cloned.1.call-update) | async-done | bytes 262160 | tf_op jit(solution)/shard_map/while/body/eval_jaxpr/psum | solution.py:9
  316.5 5.2 subtract_select_fusion.2
  324.8 4.6 constant_dynamic-slice_fusion.11
  329.4 31.2 %all-reduce.3.cloned.1.call-done = f32[512,128]{1,0:T(8,128)} async-done(((f32[512,128]{1,0:T(8,128)}), f32[512,128]{1,0:T(8,128)}) %all-reduce.3.cloned.1.call-update) | async-done | bytes 262160 | tf_op jit(solution)/shard_map/while/body/eval_jaxpr/psum | solution.py:9
  360.6 5.2 subtract_select_fusion.2
  369.0 4.6 constant_dynamic-slice_fusion.11
  373.6 31.7 %all-reduce.3.cloned.1.call-done = f32[512,128]{1,0:T(8,128)} async-done(((f32[512,128]{1,0:T(8,128)}), f32[512,128]{1,0:T(8,128)}) %all-reduce.3.cloned.1.call-update) | async-done | bytes 262160 | tf_op jit(solution)/shard_map/while/body/eval_jaxpr/psum | solution.py:9
  405.4 5.2 subtract_select_fusion.2
  410.6 180.9 %while.32 = (s32[]{:T(128)}, f32[4,512,128]{2,1,0:T(8,128)S(1)}, s32[]{:T(128)}, f32[512,4096]{1,0:T(8,128)}, f32[1536,4096]{1,0:T(8,128)}, /*index=5*/s32[]{:T(...) while((s32[]{:T(128)}, f32[4,512,128]{2,1,0:T(8,128)S(1)}, ...), condition=%wide.region_5.6_spmd, body=%wide.region_3.5_spmd.sunk | while | flops 1611464704 | bytes 22544948 | solution.py:70
  411.0 3.2 convolution_select_fusion.5
  416.5 34.3 %all-reduce.5.cloned.1.call-done = f32[512,128]{1,0:T(8,128)} async-done(((f32[512,128]{1,0:T(8,128)}), f32[512,128]{1,0:T(8,128)}) %all-reduce.5.cloned.1.call-update) | async-done | bytes 262160 | tf_op jit(solution)/shard_map/while/body/eval_jaxpr/psum | solution.py:9
  453.4 3.9 fusion.56
  457.6 3.2 convolution_select_fusion.5
  463.1 32.4 %all-reduce.5.cloned.1.call-done = f32[512,128]{1,0:T(8,128)} async-done(((f32[512,128]{1,0:T(8,128)}), f32[512,128]{1,0:T(8,128)}) %all-reduce.5.cloned.1.call-update) | async-done | bytes 262160 | tf_op jit(solution)/shard_map/while/body/eval_jaxpr/psum | solution.py:9
  497.2 3.9 fusion.56
  501.3 3.2 convolution_select_fusion.5
  506.8 33.6 %all-reduce.5.cloned.1.call-done = f32[512,128]{1,0:T(8,128)} async-done(((f32[512,128]{1,0:T(8,128)}), f32[512,128]{1,0:T(8,128)}) %all-reduce.5.cloned.1.call-update) | async-done | bytes 262160 | tf_op jit(solution)/shard_map/while/body/eval_jaxpr/psum | solution.py:9
  542.1 3.9 fusion.56
  551.7 34.1 %all-reduce.5.cloned.1.call-done = f32[512,128]{1,0:T(8,128)} async-done(((f32[512,128]{1,0:T(8,128)}), f32[512,128]{1,0:T(8,128)}) %all-reduce.5.cloned.1.call-update) | async-done | bytes 262160 | tf_op jit(solution)/shard_map/while/body/eval_jaxpr/psum | solution.py:9
  587.6 3.9 fusion.56
  (105 shorter events, 58.3 us)
Async XLA Ops:
  6.5 170.7 %all-gather.5.cloned.1.call-start = ((), (), s32[]{:S(2)}) async-start(), calls=%async_computation.2 | async-start | bytes 37748736 | tf_op jit(solution)/shard_map/all_gather | solution.py:55
  7.3 226.5 %all-gather.3.cloned.1.call-start = ((), (), s32[]{:S(2)}) async-start(), calls=%async_computation.1 | async-start | bytes 9437184 | tf_op jit(solution)/shard_map/all_gather | solution.py:56
  56.6 3.8 copy-start.2
  64.1 25.7 %all-to-all-start = ((f32[8,1,32768]{2,1,0:T(1,128)}), f32[8,1,32768]{2,1,0:T(1,128)S(1)}, u32[]{:S(2)}, u32[]{:S(2)}) async-start(f32[8,1,32768]{2,1,0:T(1,128)} %reshape.78), calls=%async_computation | async-start | bytes 2097152 | tf_op jit(solution)/shard_map/all_to_all | solution.py:21
  233.7 38.8 %all-reduce.3.cloned.1.call-start = ((), (), s32[]{:S(2)}) async-start(), calls=%async_computation.3 | async-start | bytes 524288 | tf_op jit(solution)/shard_map/while/body/eval_jaxpr/psum | solution.py:9
  278.7 37.7 %all-reduce.3.cloned.1.call-start = ((), (), s32[]{:S(2)}) async-start(), calls=%async_computation.3 | async-start | bytes 524288 | tf_op jit(solution)/shard_map/while/body/eval_jaxpr/psum | solution.py:9
  321.7 38.9 %all-reduce.3.cloned.1.call-start = ((), (), s32[]{:S(2)}) async-start(), calls=%async_computation.3 | async-start | bytes 524288 | tf_op jit(solution)/shard_map/while/body/eval_jaxpr/psum | solution.py:9
  365.9 39.4 %all-reduce.3.cloned.1.call-start = ((), (), s32[]{:S(2)}) async-start(), calls=%async_computation.3 | async-start | bytes 524288 | tf_op jit(solution)/shard_map/while/body/eval_jaxpr/psum | solution.py:9
  410.9 3.4 copy-start
  410.9 39.9 %all-reduce.5.cloned.1.call-start = ((), (), s32[]{:S(2)}) async-start(), calls=%async_computation.4 | async-start | bytes 524288 | tf_op jit(solution)/shard_map/while/body/eval_jaxpr/psum | solution.py:9
  457.5 3.4 copy-start
  457.5 38.0 %all-reduce.5.cloned.1.call-start = ((), (), s32[]{:S(2)}) async-start(), calls=%async_computation.4 | async-start | bytes 524288 | tf_op jit(solution)/shard_map/while/body/eval_jaxpr/psum | solution.py:9
  501.2 3.4 copy-start
  501.2 39.2 %all-reduce.5.cloned.1.call-start = ((), (), s32[]{:S(2)}) async-start(), calls=%async_computation.4 | async-start | bytes 524288 | tf_op jit(solution)/shard_map/while/body/eval_jaxpr/psum | solution.py:9
  546.1 3.4 copy-start
  546.1 39.7 %all-reduce.5.cloned.1.call-start = ((), (), s32[]{:S(2)}) async-start(), calls=%async_computation.4 | async-start | bytes 524288 | tf_op jit(solution)/shard_map/while/body/eval_jaxpr/psum | solution.py:9
  591.6 1.0 copy-start.1
Sparse Core Ops, SparseCore 0:
  9.2 168.0 all-gather.4
  179.2 54.5 all-gather.2
  236.9 35.5 all-reduce.2
  281.9 34.5 all-reduce.2
  324.9 35.6 all-reduce.2
  369.1 36.2 all-reduce.2
  414.3 36.4 all-reduce.4
  460.9 34.5 all-reduce.4
  504.7 35.6 all-reduce.4
  549.6 36.2 all-reduce.4
where the time goes:
time: 601 us; the launch traced here: 599 us
  waiting for transfers between devices  400 us (67%)
  local copies, waits for them, and re-layouts  64.2 us (11%)
  matrix products  64.1 us (11%)
  other arithmetic  50.3 us (8%)
  between operations  13.6 us (2%)
    psum x8, waiting for transfers between devices, broadcast(): return lax.psum(block, axis)  258 us
    all_gather x1, waiting for transfers between devices, on_device(): lax.all_gather(tri_panels, 'col', axis=1, tiled=True)  81.6 us
    another operation x4, other arithmetic, on_device(): jax.scipy.linalg.solve_triangular(own_diag, identity_block, lower=True)  41.7 us
    all_gather x1, waiting for transfers between devices, on_device(): lax.all_gather(own_inverse, 'col', axis=1, tiled=True)  39 us
    dot_general x8, matrix products, advance(): jnp.einsum('sij,jc->sic', pieces, solution, precision=lax.Precision.HIGHEST)  36.6 us
    dynamic_slice x8, local copies, waits for them, and re-layouts, upfront_step(): lax.dynamic_slice_in_dim(own_rows, step_index * block_size, block_size, 1)  27.3 us
    dot_general x8, matrix products, advance(): jnp.dot(inverse_block, current, precision=lax.Precision.HIGHEST, preferre...  24.5 us
    all_to_all x1, waiting for transfers between devices, on_device(): lax.all_to_all(parted, 'col', split_axis=2, concat_axis=1, tiled=True)  20.5 us
  transfers between devices with their start and end apart: 11, of which 11 were waited for; matrix products, arithmetic and copies ran while one was open for 18% of the time, Pallas kernels for 0%

commit v1 on v0

--- a/solution.py
+++ b/solution.py
@@ -6,7 +6,7 @@
 
 def broadcast(block, axis, source):
     block = jnp.where(lax.axis_index(axis) == source, block, jnp.zeros_like(block))
-    return lax.psum(block, axis)
+    return jnp.sum(lax.all_gather(block, axis), axis=0)
 
 
 def on_device(tri_panels, rhs_rows):

time: 601 us -> 548 us (0.912)
  waiting for transfers between devices: 400 us -> 335 us
  other arithmetic: 50.3 us -> 62.8 us
    psum x8 -> x0, waiting for transfers between devices: 258 us -> none  [broadcast(): return lax.psum(block, axis)]
    all_gather x0 -> x8, waiting for transfers between devices: none -> 193 us  [broadcast(): return jnp.sum(lax.all_gather(block, axis), axis=0)]
    reduce_sum x0 -> x8, other arithmetic: none -> 10.4 us  [broadcast(): return jnp.sum(lax.all_gather(block, axis), axis=0)]
  transfers between devices with their start and end apart: 11 -> 11, of which waited for: 11 -> 11; matrix products, arithmetic and copies ran while one was open for 18% -> 20% of each run, Pallas kernels for 0% -> 0%
where the time goes in v1:
time: 548 us; the launch traced here: 546 us
  waiting for transfers between devices  335 us (61%)
  local copies, waits for them, and re-layouts  64 us (12%)
  matrix products  63.8 us (12%)
  other arithmetic  62.8 us (11%)
  between operations  13.6 us (2%)
  starting transfers between devices  5.55 us (1%)
    all_gather x8, waiting for transfers between devices, broadcast(): return jnp.sum(lax.all_gather(block, axis), axis=0)  193 us
    all_gather x1, waiting for transfers between devices, on_device(): lax.all_gather(tri_panels, 'col', axis=1, tiled=True)  81.6 us
    another operation x4, other arithmetic, on_device(): jax.scipy.linalg.solve_triangular(own_diag, identity_block, lower=True)  41.7 us
    all_gather x1, waiting for transfers between devices, on_device(): lax.all_gather(own_inverse, 'col', axis=1, tiled=True)  39 us
    dot_general x8, matrix products, advance(): jnp.einsum('sij,jc->sic', pieces, solution, precision=lax.Precision.HIGHEST)  36.3 us
    dynamic_slice x8, local copies, waits for them, and re-layouts, upfront_step(): lax.dynamic_slice_in_dim(own_rows, step_index * block_size, block_size, 1)  27.3 us
    dot_general x8, matrix products, advance(): jnp.dot(inverse_block, current, precision=lax.Precision.HIGHEST, preferre...  24.5 us
    all_to_all x1, waiting for transfers between devices, on_device(): lax.all_to_all(parted, 'col', split_axis=2, concat_axis=1, tiled=True)  20.5 us
  transfers between devices with their start and end apart: 11, of which 11 were waited for; matrix products, arithmetic and copies ran while one was open for 20% of the time, Pallas kernels for 0%

profile of v1, /device:TPU:0, one launch (start us, length us, event | category | flops | bytes accessed | tf_op | source)
XLA Modules:
  0.0 546.0 jit_solution(10618110369291965884)
XLA Ops:
  8.7 8.0 %while.33 = (s32[]{:T(128)}, f32[512,512]{1,0:T(8,128)S(1)}, s32[4,2]{0,1:T(2,128)S(1)}, f32[4,128,128]{2,1,0:T(8,128)S(1)}, s32[]{:T(128)}) while((s32[]{:T(128)}, f32[512,512]{1,0:T(8,128)S(1)}, s32[4,2]{0,1:T(2,128)S(1)}, f32[4,128,128]{2,1,0:T(8,128)S(1)}, s32[]{:T(128)}) %tuple.81), condition=%wide.while_cond, body=%wide.while_body.sunk | while | flops 2 | bytes 131181 | solution.py:26
  16.7 39.3 %custom-call.4 = f32[4,128,128]{1,2,0:T(8,128)S(1)} custom-call(f32[4,128,128]{2,1,0:T(8,128)S(1)} %get-tuple-element.284), custom_call_target="InvertDiagBlocksLowerTriangular" | custom-call | tf_op jit(solution)/shard_map/jit(_solve_triangular)/triangular_solve | solution.py:26
  64.1 5.2 all-to-all-start
  69.3 20.5 %all-to-all-done = f32[8,1,32768]{2,1,0:T(1,128)S(1)} async-done(((f32[8,1,32768]{2,1,0:T(1,128)}), f32[8,1,32768]{2,1,0:T(1,128)S(1)}, u32[]{:S(2)}, u32[]{:S(2)}) %all-to-all-start) | async-done | bytes 1048608 | tf_op jit(solution)/shard_map/all_to_all | solution.py:21
  95.7 81.6 %all-gather.13.cloned.1.call-done = f32[2048,4096]{1,0:T(8,128)} async-done(((f32[2048,512]{1,0:T(8,128)}), f32[2048,4096]{1,0:T(8,128)}) %all-gather.13.cloned.1.call-update) | async-done | bytes 33554448 | tf_op jit(solution)/shard_map/all_gather | solution.py:55
  177.3 17.5 %slice.70 = f32[1536,4096]{1,0:T(8,128)} slice(f32[2048,4096]{1,0:T(8,128)} %all-gather.13.cloned.1.call-done), slice={[512:2048], [0:4096]} | slice | bytes 50331648 | tf_op jit(solution)/shard_map/slice | solution.py:61
  194.7 39.0 %all-gather.11.cloned.1.call-done = f32[512,4096]{1,0:T(8,128)} async-done(((f32[512,512]{1,0:T(8,128)}), f32[512,4096]{1,0:T(8,128)}) %all-gather.11.cloned.1.call-update) | async-done | bytes 8388624 | tf_op jit(solution)/shard_map/all_gather | solution.py:56
  233.7 149.2 %while.31 = (s32[]{:T(128)}, f32[4,512,128]{2,1,0:T(8,128)S(1)}, s32[]{:T(128)}, f32[512,4096]{1,0:T(8,128)}, f32[2048,4096]{1,0:T(8,128)}, /*index=5*/s32[]{:T(...) while((s32[]{:T(128)}, f32[4,512,128]{2,1,0:T(8,128)S(1)}, ...), condition=%wide.region_2.3_spmd, body=%wide.region_0.2_spmd.sunk | while | flops 2014117888 | bytes 22544856 | solution.py:70
  236.7 4.6 constant_dynamic-slice_fusion.6
  241.3 23.5 %all-gather.15.cloned.1.call-done = f32[2048,128]{1,0:T(8,128)} async-done(((f32[512,128]{1,0:T(8,128)}), f32[2048,128]{1,0:T(8,128)}) %all-gather.15.cloned.1.call-update) | async-done | bytes 1048592 | tf_op jit(solution)/shard_map/while/body/eval_jaxpr/all_gather | solution.py:9
  266.2 5.2 subtract_select_fusion.2
  274.5 4.6 constant_dynamic-slice_fusion.6
  279.1 22.9 %all-gather.15.cloned.1.call-done = f32[2048,128]{1,0:T(8,128)} async-done(((f32[512,128]{1,0:T(8,128)}), f32[2048,128]{1,0:T(8,128)}) %all-gather.15.cloned.1.call-update) | async-done | bytes 1048592 | tf_op jit(solution)/shard_map/while/body/eval_jaxpr/all_gather | solution.py:9
  303.3 5.2 subtract_select_fusion.2
  311.6 4.6 constant_dynamic-slice_fusion.6
  316.3 22.9 %all-gather.15.cloned.1.call-done = f32[2048,128]{1,0:T(8,128)} async-done(((f32[512,128]{1,0:T(8,128)}), f32[2048,128]{1,0:T(8,128)}) %all-gather.15.cloned.1.call-update) | async-done | bytes 1048592 | tf_op jit(solution)/shard_map/while/body/eval_jaxpr/all_gather | solution.py:9
  340.5 5.2 subtract_select_fusion.2
  348.8 4.6 constant_dynamic-slice_fusion.6
  353.4 22.9 %all-gather.15.cloned.1.call-done = f32[2048,128]{1,0:T(8,128)} async-done(((f32[512,128]{1,0:T(8,128)}), f32[2048,128]{1,0:T(8,128)}) %all-gather.15.cloned.1.call-update) | async-done | bytes 1048592 | tf_op jit(solution)/shard_map/while/body/eval_jaxpr/all_gather | solution.py:9
  377.6 5.2 subtract_select_fusion.2
  382.9 155.3 %while.32 = (s32[]{:T(128)}, f32[4,512,128]{2,1,0:T(8,128)S(1)}, s32[]{:T(128)}, f32[512,4096]{1,0:T(8,128)}, f32[1536,4096]{1,0:T(8,128)}, /*index=5*/s32[]{:T(...) while((s32[]{:T(128)}, f32[4,512,128]{2,1,0:T(8,128)S(1)}, ...), condition=%wide.region_5.6_spmd, body=%wide.region_3.5_spmd.sunk | while | flops 1611595776 | bytes 25690684 | solution.py:70
  383.2 3.2 convolution_select_fusion.5
  388.7 25.3 %all-gather.17.cloned.1.call-done = f32[2048,128]{1,0:T(8,128)} async-done(((f32[512,128]{1,0:T(8,128)}), f32[2048,128]{1,0:T(8,128)}) %all-gather.17.cloned.1.call-update) | async-done | bytes 1048592 | tf_op jit(solution)/shard_map/while/body/eval_jaxpr/all_gather | solution.py:9
  418.0 3.8 fusion.62
  422.0 3.2 convolution_select_fusion.5
  427.5 25.3 %all-gather.17.cloned.1.call-done = f32[2048,128]{1,0:T(8,128)} async-done(((f32[512,128]{1,0:T(8,128)}), f32[2048,128]{1,0:T(8,128)}) %all-gather.17.cloned.1.call-update) | async-done | bytes 1048592 | tf_op jit(solution)/shard_map/while/body/eval_jaxpr/all_gather | solution.py:9
  456.7 3.8 fusion.62
  466.2 25.3 %all-gather.17.cloned.1.call-done = f32[2048,128]{1,0:T(8,128)} async-done(((f32[512,128]{1,0:T(8,128)}), f32[2048,128]{1,0:T(8,128)}) %all-gather.17.cloned.1.call-update) | async-done | bytes 1048592 | tf_op jit(solution)/shard_map/while/body/eval_jaxpr/all_gather | solution.py:9
  495.5 3.8 fusion.62
  499.5 3.2 convolution_select_fusion.5
  505.0 25.3 %all-gather.17.cloned.1.call-done = f32[2048,128]{1,0:T(8,128)} async-done(((f32[512,128]{1,0:T(8,128)}), f32[2048,128]{1,0:T(8,128)}) %all-gather.17.cloned.1.call-update) | async-done | bytes 1048592 | tf_op jit(solution)/shard_map/while/body/eval_jaxpr/all_gather | solution.py:9
  534.2 3.8 fusion.62
  (105 shorter events, 70.5 us)
Async XLA Ops:
  6.5 170.7 %all-gather.13.cloned.1.call-start = ((), (), s32[]{:S(2)}) async-start(), calls=%async_computation.2 | async-start | bytes 37748736 | tf_op jit(solution)/shard_map/all_gather | solution.py:55
  7.3 226.5 %all-gather.11.cloned.1.call-start = ((), (), s32[]{:S(2)}) async-start(), calls=%async_computation.1 | async-start | bytes 9437184 | tf_op jit(solution)/shard_map/all_gather | solution.py:56
  56.6 3.8 copy-start.2
  64.1 25.7 %all-to-all-start = ((f32[8,1,32768]{2,1,0:T(1,128)}), f32[8,1,32768]{2,1,0:T(1,128)S(1)}, u32[]{:S(2)}, u32[]{:S(2)}) async-start(f32[8,1,32768]{2,1,0:T(1,128)} %reshape.92), calls=%async_computation | async-start | bytes 2097152 | tf_op jit(solution)/shard_map/all_to_all | solution.py:21
  233.7 31.1 %all-gather.15.cloned.1.call-start = ((), (), s32[]{:S(2)}) async-start(), calls=%async_computation.3 | async-start | bytes 1310720 | tf_op jit(solution)/shard_map/while/body/eval_jaxpr/all_gather | solution.py:9
  271.4 30.5 %all-gather.15.cloned.1.call-start = ((), (), s32[]{:S(2)}) async-start(), calls=%async_computation.3 | async-start | bytes 1310720 | tf_op jit(solution)/shard_map/while/body/eval_jaxpr/all_gather | solution.py:9
  308.6 30.5 %all-gather.15.cloned.1.call-start = ((), (), s32[]{:S(2)}) async-start(), calls=%async_computation.3 | async-start | bytes 1310720 | tf_op jit(solution)/shard_map/while/body/eval_jaxpr/all_gather | solution.py:9
  345.7 30.5 %all-gather.15.cloned.1.call-start = ((), (), s32[]{:S(2)}) async-start(), calls=%async_computation.3 | async-start | bytes 1310720 | tf_op jit(solution)/shard_map/while/body/eval_jaxpr/all_gather | solution.py:9
  383.1 3.4 copy-start
  383.1 30.8 %all-gather.17.cloned.1.call-start = ((), (), s32[]{:S(2)}) async-start(), calls=%async_computation.4 | async-start | bytes 1310720 | tf_op jit(solution)/shard_map/while/body/eval_jaxpr/all_gather | solution.py:9
  421.9 3.4 copy-start
  421.9 30.8 %all-gather.17.cloned.1.call-start = ((), (), s32[]{:S(2)}) async-start(), calls=%async_computation.4 | async-start | bytes 1310720 | tf_op jit(solution)/shard_map/while/body/eval_jaxpr/all_gather | solution.py:9
  460.6 3.4 copy-start
  460.7 30.8 %all-gather.17.cloned.1.call-start = ((), (), s32[]{:S(2)}) async-start(), calls=%async_computation.4 | async-start | bytes 1310720 | tf_op jit(solution)/shard_map/while/body/eval_jaxpr/all_gather | solution.py:9
  499.4 3.4 copy-start
  499.4 30.8 %all-gather.17.cloned.1.call-start = ((), (), s32[]{:S(2)}) async-start(), calls=%async_computation.4 | async-start | bytes 1310720 | tf_op jit(solution)/shard_map/while/body/eval_jaxpr/all_gather | solution.py:9
  538.2 1.0 copy-start.1
Sparse Core Ops, SparseCore 0:
  9.2 168.0 all-gather.12
  179.2 54.5 all-gather.10
  236.8 27.9 all-gather.14
  274.6 27.3 all-gather.14
  311.7 27.3 all-gather.14
  348.9 27.3 all-gather.14
  386.6 27.3 all-gather.16
  425.4 27.3 all-gather.16
  464.1 27.3 all-gather.16
  502.9 27.3 all-gather.16
